TPU v7x, 32 devices: a whole 2x2x4 slice. The times are simulated.
32 devices in a mesh: row: 4 (over y, x), col: 8 (over z, core).
Axes of the slice: x: 2, y: 2, z: 4, core: 2. Of those that a mesh axis runs over, the one named last changes fastest.
Arguments:
- residuals: bfloat16 [32768, 768], P(('row', 'col')), may hold values from -6 to 6
- codes: int32 [32768, 64], P(('row', 'col')), may hold values from 0 to 255
- list_ids: int32 [32768], P(('row', 'col')), may hold values from 0 to 8191, as said below
- rotation: bfloat16 [768, 768], replicated, may hold values from -0.21875 to 0.21875
- codebook: bfloat16 [256, 768], replicated, may hold values from -6 to 6
- list_fill: int32 [8192], P(('row', 'col')), may hold values from 0 to 4095
Outputs:
- list_drift: float32 [8192, 768], P(('row', 'col'))
- list_counts: int32 [8192], P(('row', 'col'))
- new_blocks: int32 [8192], P(('row', 'col'))
Inputs may be any that keep to these rules, and one draw needn't show every extreme that they name: `list_ids`: lists are grouped in blocks of 256 consecutive ids. Among the rows of one device (aligned blocks of 1024 rows), at most 96 have lists in the same block, and in every such aligned block some list block is named by exactly 96 rows.
All inputs are finite; a program needn't handle non-finite values.
Results may differ from a plain program's by a relative error of at most 0.0029.
Values may be sent and summed in bfloat16 or wider, within the bound.
No kernel may reach another device: no remote copies, remote signals or barrier semaphores. Data moves between devices by JAX's collectives and lax.ppermute only.
A program may use at most 64 MiB of HBM per device.

v0:
```python
import jax
import jax.numpy as jnp
from jax import lax
from jax.sharding import PartitionSpec as P


def decode_rows(codes, codebook):
    vec_rows, sub_count = codes.shape
    cent_count, feat_width = codebook.shape
    sub_width = feat_width // sub_count
    code_table = codebook.reshape(cent_count, sub_count, sub_width)
    block_rows = 256
    code_blocks = codes.reshape(vec_rows // block_rows, block_rows, sub_count)

    def one_block(code_block):
        picker = (
            code_block[:, :, None] == jnp.arange(cent_count, dtype=jnp.int32)[None, None, :]
        ).astype(jnp.bfloat16)
        picked = jnp.einsum("bmk,kmj->bmj", picker, code_table, preferred_element_type=jnp.float32)
        return picked.reshape(block_rows, feat_width)

    return lax.map(one_block, code_blocks).reshape(vec_rows, feat_width)


def sum_by_list(rows_in, tags_in, list_total):
    picker = (tags_in[:, None] == jnp.arange(list_total, dtype=jnp.int32)[None, :]).astype(
        jnp.bfloat16
    )
    list_sums = lax.dot_general(
        picker, rows_in, (((0,), (0,)), ((), ())), preferred_element_type=jnp.float32
    )
    counts = jnp.sum(picker, axis=0, dtype=jnp.float32)
    return (list_sums, counts)


def rank_in_block(owner_block, owner_total):
    vec_rows = owner_block.shape[0]
    picker = (owner_block[:, None] == jnp.arange(owner_total, dtype=jnp.int32)[None, :]).astype(
        jnp.bfloat16
    )
    later = (
        jnp.arange(vec_rows, dtype=jnp.int32)[:, None]
        > jnp.arange(vec_rows, dtype=jnp.int32)[None, :]
    )
    before = jnp.dot(later.astype(jnp.bfloat16), picker, preferred_element_type=jnp.float32)
    return jnp.sum(before * picker.astype(jnp.float32), axis=1).astype(jnp.int32)


def local(residuals, codes, list_ids, rotation, codebook, list_fill):
    row_count = lax.axis_size("row")
    col_count = lax.axis_size("col")
    owner_total = row_count * col_count
    vec_rows, feat_width = residuals.shape
    lists_here = list_fill.shape[0]
    slot_cap = 3 * vec_rows // owner_total
    rotated = jnp.dot(residuals, rotation, preferred_element_type=jnp.float32)
    rebuilt = decode_rows(codes, codebook)
    encode_error = (rotated - rebuilt).astype(jnp.bfloat16)
    owner_block = list_ids // lists_here
    slot_index = owner_block * slot_cap + rank_in_block(owner_block, owner_total)
    send_rows = (
        jnp.zeros((owner_total * slot_cap, feat_width), jnp.bfloat16)
        .at[slot_index]
        .set(encode_error)
    )
    send_tags = jnp.full((owner_total * slot_cap,), -1, jnp.int32).at[slot_index].set(list_ids)
    send_rows = send_rows.reshape(row_count, col_count, slot_cap, feat_width)
    send_tags = send_tags.reshape(row_count, col_count, slot_cap)
    got_rows, got_tags = (
        lax.all_to_all(
            lax.all_to_all(send_rows, "row", split_axis=0, concat_axis=0, tiled=True),
            "col",
            split_axis=1,
            concat_axis=1,
            tiled=True,
        ),
        lax.all_to_all(
            lax.all_to_all(send_tags, "row", split_axis=0, concat_axis=0, tiled=True),
            "col",
            split_axis=1,
            concat_axis=1,
            tiled=True,
        ),
    )
    got_rows = got_rows.reshape(-1, feat_width)
    got_tags = got_tags.reshape(-1)
    list_base = (lax.axis_index("row") * col_count + lax.axis_index("col")) * lists_here
    local_index = jnp.where(got_tags >= 0, got_tags - list_base, -1)
    list_sums, counts = sum_by_list(got_rows, local_index, lists_here)
    list_counts = counts.astype(jnp.int32)
    divisor = jnp.maximum(list_counts, 1).astype(jnp.float32)
    list_drift = list_sums / divisor[:, None]
    new_blocks = (list_fill + list_counts + 127) // 128 - (list_fill + 127) // 128
    return (list_drift, list_counts, new_blocks)


def solution(mesh):
    placed = (
        P(("row", "col"), None),
        P(("row", "col"), None),
        P(("row", "col")),
        P(),
        P(),
        P(("row", "col")),
    )
    return jax.shard_map(
        local,
        mesh=mesh,
        in_specs=placed,
        out_specs=(P(("row", "col"), None), P(("row", "col")), P(("row", "col"))),
        check_vma=False,
    )
```

profile of v0, /device:TPU:0, one launch (start us, length us, event | category | flops | bytes accessed | tf_op | source)
XLA Modules:
  0.0 245.6 jit_solution(13785492173893013077)
XLA Ops:
  0.6 0.0 copy-start
  0.6 0.8 add_select_fusion
  1.5 0.5 fusion.12
  2.0 0.7 compare_select_fusion
  2.7 4.5 %scatter_custom_fusion = s32[3072]{0:T(1024)S(1)} fusion(s32[1024]{0:T(1024)S(1)} %compare_select_fusion, s32[1024]{0:T(1024)} %param.10, s32[]{:T(128)} %constant.57.clone.1), kind=kCustom, calls=%fused_computation.32 | custom fusion | bytes 12800 | tf_op jit(solution)/shard_map/scatter | solution.py:66
  7.2 0.7 reshape.51
  7.9 5.2 %all-to-all-start = ((s32[4,8,96]{2,1,0:T(8,128)}), s32[4,8,96]{2,1,0:T(8,128)S(1)}, u32[]{:S(2)}, u32[]{:S(2)}) async-start(s32[4,8,96]{2,1,0:T(8,128)} %reshape.51), calls=%async_computation | async-start | bytes 32768 | tf_op jit(solution)/shard_map/all_to_all | solution.py:78
  13.1 1.8 reshape.52
  14.8 1.2 copy.26
  16.0 0.9 reshape.53
  16.9 32.8 %while.10 = (s32[]{:T(128)}, f32[4,256,768]{2,1,0:T(8,128)}, s32[4,256,64]{1,0,2:T(4,128)}, bf16[256,64,12]{0,2,1:T(8,128)(2,1)}, s32[]{:T(128)}) while((s32[]{:T(128)}, f32[4,256,768]{2,1,0:T(8,128)}, s32[4,256,64]{1,0,2:T(4,128)}, bf16[256,64,12]{0,2,1:T(8,128)(2,1)}, s32[]{:T(128)}) %tuple.27), condition=%wide.region_3.4_spmd, body=%wide.region_2.3_spmd.sunk | while | flops 104857600 | bytes 6225997 | solution.py:22
  16.9 1.0 constant_dynamic-slice_fusion.2
  17.9 5.9 %fusion.27 = f32[256,64,12]{0,2,1:T(8,128)S(1)} fusion(bf16[256,64,12]{0,2,1:T(8,128)(2,1)} %get-tuple-element.90, s32[256,64]{0,1:T(8,128)S(1)} %bitcast.29), kind=kOutput, calls=%fused_computation.5.clone.1 | convolution fusion | flops 104857600 | bytes 1245184 | tf_op jit(solution)/shard_map/while/body/eval_jaxpr/bmk,kmj->bmj/dot_general | solution.py:19
  23.8 0.1 broadcast_in_dim.41
  23.9 0.3 copy.41
  24.1 0.9 constant_dynamic-update-slice_fusion.2
  25.1 1.0 constant_dynamic-slice_fusion.2
  26.1 5.9 %fusion.27 = f32[256,64,12]{0,2,1:T(8,128)S(1)} fusion(bf16[256,64,12]{0,2,1:T(8,128)(2,1)} %get-tuple-element.90, s32[256,64]{0,1:T(8,128)S(1)} %bitcast.29), kind=kOutput, calls=%fused_computation.5.clone.1 | convolution fusion | flops 104857600 | bytes 1245184 | tf_op jit(solution)/shard_map/while/body/eval_jaxpr/bmk,kmj->bmj/dot_general | solution.py:19
  32.0 0.1 broadcast_in_dim.41
  32.1 0.3 copy.41
  32.3 0.9 constant_dynamic-update-slice_fusion.2
  33.3 1.0 constant_dynamic-slice_fusion.2
  34.3 5.9 %fusion.27 = f32[256,64,12]{0,2,1:T(8,128)S(1)} fusion(bf16[256,64,12]{0,2,1:T(8,128)(2,1)} %get-tuple-element.90, s32[256,64]{0,1:T(8,128)S(1)} %bitcast.29), kind=kOutput, calls=%fused_computation.5.clone.1 | convolution fusion | flops 104857600 | bytes 1245184 | tf_op jit(solution)/shard_map/while/body/eval_jaxpr/bmk,kmj->bmj/dot_general | solution.py:19
  40.2 0.1 broadcast_in_dim.41
  40.3 0.3 copy.41
  40.5 1.0 constant_dynamic-update-slice_fusion.2
  41.5 1.0 constant_dynamic-slice_fusion.2
  42.5 5.9 %fusion.27 = f32[256,64,12]{0,2,1:T(8,128)S(1)} fusion(bf16[256,64,12]{0,2,1:T(8,128)(2,1)} %get-tuple-element.90, s32[256,64]{0,1:T(8,128)S(1)} %bitcast.29), kind=kOutput, calls=%fused_computation.5.clone.1 | convolution fusion | flops 104857600 | bytes 1245184 | tf_op jit(solution)/shard_map/while/body/eval_jaxpr/bmk,kmj->bmj/dot_general | solution.py:19
  48.4 0.1 broadcast_in_dim.41
  48.5 0.3 copy.41
  48.7 0.9 constant_dynamic-update-slice_fusion.2
  49.7 0.0 copy-done
  49.7 3.6 %fusion.4 = bf16[1024,768]{1,0:T(8,128)(2,1)S(1)} fusion(f32[4,256,768]{2,1,0:T(8,128)} %get-tuple-element.25, bf16[1024,768]{1,0:T(8,128)(2,1)S(1)} %copy-done, bf16[768,768]{1,0:T(8,128)(2,1)} %param.11), kind=kOutput, calls=%fused_computation.12 | convolution fusion | flops 1209532416 | bytes 7471104 | tf_op jit(solution)/shard_map/dot_general | solution.py:56
  53.3 8.2 %scatter_custom_fusion.1 = bf16[3072,768]{1,0:T(8,128)(2,1)} fusion(s32[1024]{0:T(1024)S(1)} %compare_select_fusion, bf16[1024,768]{1,0:T(8,128)(2,1)S(1)} %fusion.4, bf16[]{:T(256)} %constant.68.clone.1), kind=kCustom, calls=%fused_computation.17 | custom fusion | bytes 4718594 | tf_op jit(solution)/shard_map/scatter | solution.py:64
  61.5 0.0 all-to-all-done
  61.5 4.9 %all-to-all-start.2 = ((bf16[4,8,96,768]{3,2,1,0:T(8,128)(2,1)}), bf16[4,8,96,768]{3,2,1,0:T(8,128)(2,1)}, u32[]{:S(2)}, u32[]{:S(2)}) async-start(bf16[4,8,96,768]{3,2,1,0:T(8,128)(2,1)} %bitcast.27), calls=%async_computation.2 | async-start | bytes 9437184 | tf_op jit(solution)/shard_map/all_to_all | solution.py:71
  66.5 0.6 copy.24
  67.1 52.4 %all-to-all-done.2 = bf16[4,8,96,768]{3,2,1,0:T(8,128)(2,1)} async-done(((bf16[4,8,96,768]{3,2,1,0:T(8,128)(2,1)}), bf16[4,8,96,768]{3,2,1,0:T(8,128)(2,1)}, u32[]{:S(2)}, u32[]{:S(2)}) %all-to-all-start.2) | async-done | bytes 4718624 | tf_op jit(solution)/shard_map/all_to_all | solution.py:71
  119.5 4.9 %all-to-all-start.1 = ((s32[4,8,96]{2,0,1:T(4,128)}), s32[4,8,96]{2,0,1:T(4,128)S(1)}, u32[]{:S(2)}, u32[]{:S(2)}) async-start(s32[4,8,96]{2,0,1:T(4,128)} %copy.24), calls=%async_computation.1 | async-start | bytes 32768 | tf_op jit(solution)/shard_map/all_to_all | solution.py:77
  124.4 4.9 %copy.29 = bf16[4,8,96,768]{3,2,0,1:T(8,128)(2,1)} copy(bf16[4,8,96,768]{3,2,1,0:T(8,128)(2,1)} %all-to-all-done.2) | data formatting | bytes 9437184 | tf_op jit(solution)/shard_map/all_to_all | solution.py:71
  129.3 0.0 copy-start.2
  129.3 0.8 all-to-all-done.1
  130.0 4.8 %all-to-all-start.3 = ((bf16[4,8,96,768]{3,2,0,1:T(8,128)(2,1)}), bf16[4,8,96,768]{3,2,0,1:T(8,128)(2,1)}, u32[]{:S(2)}, u32[]{:S(2)}) async-start(bf16[4,8,96,768]{3,2,0,1:T(8,128)(2,1)} %copy.29), calls=%async_computation.3 | async-start | bytes 9437184 | tf_op jit(solution)/shard_map/all_to_all | solution.py:70
  134.9 0.1 select_n.31
  134.9 1.4 convert_reduce_fusion
  136.3 0.0 copy-done.2
  136.3 0.6 fusion.19
  136.9 0.0 copy-start.1
  136.9 103.0 %all-to-all-done.3 = bf16[4,8,96,768]{3,2,0,1:T(8,128)(2,1)} async-done(((bf16[4,8,96,768]{3,2,0,1:T(8,128)(2,1)}), bf16[4,8,96,768]{3,2,0,1:T(8,128)(2,1)}, u32[]{:S(2)}, u32[]{:S(2)}) %all-to-all-start.3) | async-done | bytes 4718624 | tf_op jit(solution)/shard_map/all_to_all | solution.py:70
  239.9 2.7 %copy.30 = bf16[4,8,96,768]{3,2,1,0:T(8,128)(2,1)S(1)} copy(bf16[4,8,96,768]{3,2,0,1:T(8,128)(2,1)} %all-to-all-done.3) | data formatting | bytes 9437184 | tf_op jit(solution)/shard_map/all_to_all | solution.py:70
  242.6 0.0 copy-done.1
  242.6 3.0 %fusion.10 = f32[256,768]{1,0:T(8,128)} fusion(bf16[3072,768]{1,0:T(8,128)(2,1)S(1)} %bitcast.28, s32[3072]{0:T(1024)S(1)} %select_n.31, f32[256]{0:T(256)S(1)} %maximum_convert_fusion), kind=kOutput, calls=%fused_computation.20 | convolution fusion | flops 1208942592 | bytes 5518336 | tf_op jit(solution)/shard_map/dot_general | solution.py:29
  (8 shorter events, 0.0 us)
Async XLA Ops:
  0.6 49.1 %copy-start = (bf16[1024,768]{1,0:T(8,128)(2,1)S(1)}, bf16[1024,768]{1,0:T(8,128)(2,1)}, u32[]{:S(2)}) copy-start(bf16[1024,768]{1,0:T(8,128)(2,1)} %param.8) | copy-start | bytes 4718596
  7.9 53.7 %all-to-all-start = ((s32[4,8,96]{2,1,0:T(8,128)}), s32[4,8,96]{2,1,0:T(8,128)S(1)}, u32[]{:S(2)}, u32[]{:S(2)}) async-start(s32[4,8,96]{2,1,0:T(8,128)} %reshape.51), calls=%async_computation | async-start | bytes 32768 | tf_op jit(solution)/shard_map/all_to_all | solution.py:78
  61.5 58.0 %all-to-all-start.2 = ((bf16[4,8,96,768]{3,2,1,0:T(8,128)(2,1)}), bf16[4,8,96,768]{3,2,1,0:T(8,128)(2,1)}, u32[]{:S(2)}, u32[]{:S(2)}) async-start(bf16[4,8,96,768]{3,2,1,0:T(8,128)(2,1)} %bitcast.27), calls=%async_computation.2 | async-start | bytes 9437184 | tf_op jit(solution)/shard_map/all_to_all | solution.py:71
  119.5 10.5 %all-to-all-start.1 = ((s32[4,8,96]{2,0,1:T(4,128)}), s32[4,8,96]{2,0,1:T(4,128)S(1)}, u32[]{:S(2)}, u32[]{:S(2)}) async-start(s32[4,8,96]{2,0,1:T(4,128)} %copy.24), calls=%async_computation.1 | async-start | bytes 32768 | tf_op jit(solution)/shard_map/all_to_all | solution.py:77
  129.3 7.0 %copy-start.2 = (s32[256]{0:T(256)S(1)}, s32[256]{0:T(256)}, u32[]{:S(2)}) copy-start(s32[256]{0:T(256)} %param.13) | copy-start | bytes 3076
  130.0 109.8 %all-to-all-start.3 = ((bf16[4,8,96,768]{3,2,0,1:T(8,128)(2,1)}), bf16[4,8,96,768]{3,2,0,1:T(8,128)(2,1)}, u32[]{:S(2)}, u32[]{:S(2)}) async-start(bf16[4,8,96,768]{3,2,0,1:T(8,128)(2,1)} %copy.29), calls=%async_computation.3 | async-start | bytes 9437184 | tf_op jit(solution)/shard_map/all_to_all | solution.py:70
  136.9 105.7 %copy-start.1 = (s32[256]{0:T(256)}, s32[256]{0:T(256)S(1)}, u32[]{:S(2)}) copy-start(s32[256]{0:T(256)S(1)} %get-tuple-element.51) | copy-start | bytes 3076
where the time goes:
time: 247 us; the launch traced here: 246 us
  waiting for transfers between devices  156 us (63%)
  local copies, waits for them, and re-layouts  34.7 us (14%)
  matrix products  30.6 us (12%)
  starting transfers between devices  19.8 us (8%)
  other arithmetic  3.47 us (1%)
    all_to_all x1, waiting for transfers between devices, local(): lax.all_to_all(lax.all_to_all(send_rows, 'row', split_axis=0, concat_axis...  103 us
    all_to_all x1, waiting for transfers between devices, local(): lax.all_to_all(send_rows, 'row', split_axis=0, concat_axis=0, tiled=True)  52.4 us
    dot_general x4, matrix products, one_block(): jnp.einsum('bmk,kmj->bmj', picker, code_table, preferred_element_type=jnp...  23.5 us
    scatter x1, local copies, waits for them, and re-layouts, local(): send_rows = jnp.zeros((owner_total * slot_cap, feat_width), jnp.bfloat16)...  8.18 us
    all_to_all x1, starting transfers between devices, local(): lax.all_to_all(send_tags, 'row', split_axis=0, concat_axis=0, tiled=True)  5.19 us
  transfers between devices with their start and end apart: 4, of which 3 were waited for; matrix products, arithmetic and copies ran while one was open for 23% of the time, Pallas kernels for 0%

commit v1 on v0

--- a/solution.py
+++ b/solution.py
@@ -2,6 +2,18 @@
 import jax.numpy as jnp
 from jax import lax
 from jax.sharding import PartitionSpec as P
+
+
+def exchange_directly(x, axis, split, join):
+    ways, here = (lax.axis_size(axis), lax.axis_index(axis))
+    width = x.shape[split] // ways
+    turned = jnp.roll(x, -here * width, axis=split)
+    got = [lax.slice_in_dim(turned, 0, width, axis=split)]
+    for far in range(1, ways):
+        sent = lax.slice_in_dim(turned, far * width, (far + 1) * width, axis=split)
+        got.append(lax.ppermute(sent, axis, [(d, (d + far) % ways) for d in range(ways)]))
+    line = jnp.concatenate(got[::-1], axis=join)
+    return jnp.roll(line, (here + 1) * got[0].shape[join], axis=join)
 
 
 def decode_rows(codes, codebook):
@@ -68,7 +80,7 @@
     send_tags = send_tags.reshape(row_count, col_count, slot_cap)
     got_rows, got_tags = (
         lax.all_to_all(
-            lax.all_to_all(send_rows, "row", split_axis=0, concat_axis=0, tiled=True),
+            exchange_directly(send_rows, "row", 0, 0),
             "col",
             split_axis=1,
             concat_axis=1,

time: 247 us -> 247 us (level)
  other arithmetic: 3.47 us -> 14.1 us
  waiting for transfers between devices: 156 us -> 147 us
    all_to_all x2 -> x1, waiting for transfers between devices: 155 us -> 103 us  [local(): lax.all_to_all(exchange_directly(send_rows, 'row', 0, 0), 'col', split_ax...]
    all_to_all x1, waiting for transfers between devices: 0.01 us -> 43.2 us  [local(): lax.all_to_all(send_tags, 'row', split_axis=0, concat_axis=0, tiled=True)]
    concatenate x0 -> x2, other arithmetic: none -> 10.6 us  [the longest x1 6.61 us: exchange_directly(): return jnp.roll(line, (here + 1) * got[0].shape[join], axis=join)]
    ppermute x0 -> x3, starting transfers between devices: none -> 5.06 us  [exchange_directly(): lax.ppermute(sent, axis, [(d, (d + far) % ways) for d in range(ways)])]
    all_to_all x2 -> x1, local copies, waits for them, and re-layouts: 7.57 us -> 2.69 us  [local(): lax.all_to_all(exchange_directly(send_rows, 'row', 0, 0), 'col', split_ax...]
    all_to_all x2 -> x1, starting transfers between devices: 9.72 us -> 5.22 us  [local(): lax.all_to_all(exchange_directly(send_rows, 'row', 0, 0), 'col', split_ax...]
    dynamic_slice x0 -> x1, local copies, waits for them, and re-layouts: none -> 2.53 us  [exchange_directly(): return jnp.roll(line, (here + 1) * got[0].shape[join], axis=join)]
  transfers between devices with their start and end apart: 4 -> 6, of which waited for: 3 -> 2; matrix products, arithmetic and copies ran while one was open for 23% -> 7% of each run, Pallas kernels for 0% -> 0%
where the time goes in v1:
time: 247 us; the launch traced here: 245 us
  waiting for transfers between devices  147 us (60%)
  local copies, waits for them, and re-layouts  34.2 us (14%)
  matrix products  30.6 us (12%)
  starting transfers between devices  18.8 us (8%)
  other arithmetic  14.1 us (6%)
    all_to_all x1, waiting for transfers between devices, local(): lax.all_to_all(exchange_directly(send_rows, 'row', 0, 0), 'col', split_ax...  103 us
    all_to_all x1, waiting for transfers between devices, local(): lax.all_to_all(send_tags, 'row', split_axis=0, concat_axis=0, tiled=True)  43.2 us
    dot_general x4, matrix products, one_block(): jnp.einsum('bmk,kmj->bmj', picker, code_table, preferred_element_type=jnp...  23.5 us
    scatter x1, local copies, waits for them, and re-layouts, local(): send_rows = jnp.zeros((owner_total * slot_cap, feat_width), jnp.bfloat16)...  8.14 us
    concatenate x1, other arithmetic, exchange_directly(): return jnp.roll(line, (here + 1) * got[0].shape[join], axis=join)  6.61 us
    all_to_all x1, starting transfers between devices, local(): lax.all_to_all(exchange_directly(send_rows, 'row', 0, 0), 'col', split_ax...  5.22 us
    ppermute x3, starting transfers between devices, exchange_directly(): lax.ppermute(sent, axis, [(d, (d + far) % ways) for d in range(ways)])  5.06 us
  transfers between devices with their start and end apart: 6, of which 2 were waited for; matrix products, arithmetic and copies ran while one was open for 7% of the time, Pallas kernels for 0%

profile of v1, /device:TPU:0, one launch (start us, length us, event | category | flops | bytes accessed | tf_op | source)
XLA Modules:
  0.0 245.1 jit_solution(14824163437519412516)
XLA Ops:
  0.6 0.0 copy-start
  0.7 0.8 add_select_fusion
  1.5 0.5 fusion.20
  2.0 0.7 compare_select_fusion
  2.7 1.2 copy.26
  3.9 0.9 reshape.53
  4.8 1.8 reshape.52
  6.5 32.8 %while.10 = (s32[]{:T(128)}, f32[4,256,768]{2,1,0:T(8,128)}, s32[4,256,64]{1,0,2:T(4,128)}, bf16[256,64,12]{0,2,1:T(8,128)(2,1)}, s32[]{:T(128)}) while((s32[]{:T(128)}, f32[4,256,768]{2,1,0:T(8,128)}, s32[4,256,64]{1,0,2:T(4,128)}, bf16[256,64,12]{0,2,1:T(8,128)(2,1)}, s32[]{:T(128)}) %tuple.31), condition=%wide.region_3.4_spmd, body=%wide.region_2.3_spmd.sunk | while | flops 104857600 | bytes 6226497 | solution.py:34
  6.5 1.0 constant_dynamic-slice_fusion.2
  7.6 5.9 %fusion.36 = f32[256,64,12]{0,2,1:T(8,128)S(1)} fusion(bf16[256,64,12]{0,2,1:T(8,128)(2,1)} %get-tuple-element.95, s32[256,64]{0,1:T(8,128)S(1)} %bitcast.29), kind=kOutput, calls=%fused_computation.5.clone.1 | convolution fusion | flops 104857600 | bytes 1245184 | tf_op jit(solution)/shard_map/while/body/eval_jaxpr/bmk,kmj->bmj/dot_general | solution.py:31
  13.4 0.1 broadcast_in_dim.41
  13.5 0.3 copy.41
  13.8 1.0 constant_dynamic-update-slice_fusion.2
  14.8 1.0 constant_dynamic-slice_fusion.2
  15.8 5.9 %fusion.36 = f32[256,64,12]{0,2,1:T(8,128)S(1)} fusion(bf16[256,64,12]{0,2,1:T(8,128)(2,1)} %get-tuple-element.95, s32[256,64]{0,1:T(8,128)S(1)} %bitcast.29), kind=kOutput, calls=%fused_computation.5.clone.1 | convolution fusion | flops 104857600 | bytes 1245184 | tf_op jit(solution)/shard_map/while/body/eval_jaxpr/bmk,kmj->bmj/dot_general | solution.py:31
  21.6 0.1 broadcast_in_dim.41
  21.7 0.3 copy.41
  22.0 1.0 constant_dynamic-update-slice_fusion.2
  23.0 1.0 constant_dynamic-slice_fusion.2
  24.0 5.9 %fusion.36 = f32[256,64,12]{0,2,1:T(8,128)S(1)} fusion(bf16[256,64,12]{0,2,1:T(8,128)(2,1)} %get-tuple-element.95, s32[256,64]{0,1:T(8,128)S(1)} %bitcast.29), kind=kOutput, calls=%fused_computation.5.clone.1 | convolution fusion | flops 104857600 | bytes 1245184 | tf_op jit(solution)/shard_map/while/body/eval_jaxpr/bmk,kmj->bmj/dot_general | solution.py:31
  29.9 0.1 broadcast_in_dim.41
  30.0 0.3 copy.41
  30.2 1.0 constant_dynamic-update-slice_fusion.2
  31.2 1.0 constant_dynamic-slice_fusion.2
  32.2 5.9 %fusion.36 = f32[256,64,12]{0,2,1:T(8,128)S(1)} fusion(bf16[256,64,12]{0,2,1:T(8,128)(2,1)} %get-tuple-element.95, s32[256,64]{0,1:T(8,128)S(1)} %bitcast.29), kind=kOutput, calls=%fused_computation.5.clone.1 | convolution fusion | flops 104857600 | bytes 1245184 | tf_op jit(solution)/shard_map/while/body/eval_jaxpr/bmk,kmj->bmj/dot_general | solution.py:31
  38.1 0.1 broadcast_in_dim.41
  38.2 0.3 copy.41
  38.4 0.9 constant_dynamic-update-slice_fusion.2
  39.4 0.0 copy-done
  39.4 3.6 %fusion.12 = bf16[1024,768]{1,0:T(8,128)(2,1)S(1)} fusion(f32[4,256,768]{2,1,0:T(8,128)} %get-tuple-element.26, bf16[1024,768]{1,0:T(8,128)(2,1)S(1)} %copy-done, bf16[768,768]{1,0:T(8,128)(2,1)} %param.13), kind=kOutput, calls=%fused_computation.30 | convolution fusion | flops 1209532416 | bytes 7471104 | tf_op jit(solution)/shard_map/dot_general | solution.py:68
  43.0 8.1 %scatter_custom_fusion.1 = bf16[3072,768]{1,0:T(8,128)(2,1)} fusion(s32[1024]{0:T(1024)S(1)} %compare_select_fusion, bf16[1024,768]{1,0:T(8,128)(2,1)S(1)} %fusion.12, bf16[]{:T(256)} %constant.86.clone.1), kind=kCustom, calls=%fused_computation.35 | custom fusion | bytes 4718594 | tf_op jit(solution)/shard_map/scatter | solution.py:76
  51.2 4.0 %fusion.10 = bf16[4,8,96,768]{3,2,1,0:T(8,128)(2,1)S(1)} fusion(s32[]{:T(128)S(6)} %select_n.47, bf16[4,8,96,768]{3,2,1,0:T(8,128)(2,1)} %bitcast.27), kind=kLoop, calls=%fused_computation.26 | loop fusion | flops 2359296 | bytes 9437188 | tf_op jit(solution)/shard_map/jit(_roll_dynamic)/concatenate | solution.py:10
  55.2 1.9 fusion.28
  57.0 3.9 %collective-permute-start = (bf16[1,8,96,768]{3,2,1,0:T(8,128)(2,1)}, bf16[1,8,96,768]{3,2,1,0:T(8,128)(2,1)}, u32[]{:S(2)}, u32[]{:S(2)}) collective-permute-start(bf16[1,8,96,768]{3,2,1,0:T(8,128)(2,1)} %get-tuple-element.56), channel_id=1, source_target_pairs={{0,24},{8,0},{16,8},{24,16},{1,25},{9,1},{17,9},{25,17},{2,26},{10... | collective-permute-start | bytes 3538952 | tf_op jit(solution)/shard_map/ppermute | solution.py:14
  61.0 0.5 collective-permute-start.1
  61.5 0.6 collective-permute-start.2
  62.1 4.5 %scatter_custom_fusion = s32[3072]{0:T(1024)S(1)} fusion(s32[1024]{0:T(1024)S(1)} %compare_select_fusion, s32[1024]{0:T(1024)} %param.12, s32[]{:T(128)} %constant.75.clone.1), kind=kCustom, calls=%fused_computation.50 | custom fusion | bytes 12800 | tf_op jit(solution)/shard_map/scatter | solution.py:78
  66.6 0.7 reshape.51
  67.3 3.6 %all-to-all-start = ((s32[4,8,96]{2,1,0:T(8,128)}), s32[4,8,96]{2,1,0:T(8,128)S(1)}, u32[]{:S(2)}, u32[]{:S(2)}) async-start(s32[4,8,96]{2,1,0:T(8,128)} %reshape.51), calls=%async_computation | async-start | bytes 32768 | tf_op jit(solution)/shard_map/all_to_all | solution.py:90
  70.9 43.2 %all-to-all-done = s32[4,8,96]{2,1,0:T(8,128)S(1)} async-done(((s32[4,8,96]{2,1,0:T(8,128)}), s32[4,8,96]{2,1,0:T(8,128)S(1)}, u32[]{:S(2)}, u32[]{:S(2)}) %all-to-all-start) | async-done | bytes 12320 | tf_op jit(solution)/shard_map/all_to_all | solution.py:90
  114.2 0.6 copy.24
  114.8 4.9 %all-to-all-start.1 = ((s32[4,8,96]{2,0,1:T(4,128)}), s32[4,8,96]{2,0,1:T(4,128)S(1)}, u32[]{:S(2)}, u32[]{:S(2)}) async-start(s32[4,8,96]{2,0,1:T(4,128)} %copy.24), calls=%async_computation.1 | async-start | bytes 32768 | tf_op jit(solution)/shard_map/all_to_all | solution.py:89
  119.6 0.0 collective-permute-done
  119.6 0.0 collective-permute-done.1
  119.7 0.0 collective-permute-done.2
  119.7 6.6 %fusion.6 = bf16[4,8,96,768]{3,2,1,0:T(8,128)(2,1)S(1)} fusion(s32[]{:T(128)S(6)} %select_n.49, bf16[1,8,96,768]{3,2,1,0:T(8,128)(2,1)} %collective-permute-done, bf16[1,8,96,768]{3,2,1,0:T(8,128)(2,1)} %collective-permute-done.1, bf16[1,8,96,768]{3,2,1,0:T(8,128)(2,1)} %collective-permute-done.2, bf16[1,8,96,768]{3,2,1,0:T(8,128)(2,1)S(1)} %get-tuple-element.53), kind=kLoop, calls=%fused_computation.22 | loop fusion | flops 16515072 | bytes 9437188 | tf_op jit(solution)/shard_map/jit(_roll_dynamic)/concatenate | solution.py:16
  126.3 2.5 %copy.29 = bf16[4,8,96,768]{3,2,0,1:T(8,128)(2,1)} copy(bf16[4,8,96,768]{3,2,1,0:T(8,128)(2,1)S(1)} %fusion.6) | data formatting | bytes 9437184 | tf_op jit(solution)/shard_map/jit(_roll_dynamic)/dynamic_slice | solution.py:16
  128.8 0.0 copy-start.2
  128.8 0.0 all-to-all-done.1
  128.8 5.2 %all-to-all-start.2 = ((bf16[4,8,96,768]{3,2,0,1:T(8,128)(2,1)}), bf16[4,8,96,768]{3,2,0,1:T(8,128)(2,1)}, u32[]{:S(2)}, u32[]{:S(2)}) async-start(bf16[4,8,96,768]{3,2,0,1:T(8,128)(2,1)} %copy.29), calls=%async_computation.2 | async-start | bytes 9437184 | tf_op jit(solution)/shard_map/all_to_all | solution.py:82
  134.1 0.1 select_n.41
  134.1 1.4 convert_reduce_fusion
  135.5 0.0 copy-done.2
  135.5 0.6 fusion.27
  136.1 0.0 copy-start.1
  136.1 103.3 %all-to-all-done.2 = bf16[4,8,96,768]{3,2,0,1:T(8,128)(2,1)} async-done(((bf16[4,8,96,768]{3,2,0,1:T(8,128)(2,1)}), bf16[4,8,96,768]{3,2,0,1:T(8,128)(2,1)}, u32[]{:S(2)}, u32[]{:S(2)}) %all-to-all-start.2) | async-done | bytes 4718624 | tf_op jit(solution)/shard_map/all_to_all | solution.py:82
  239.4 2.7 %copy.30 = bf16[4,8,96,768]{3,2,1,0:T(8,128)(2,1)S(1)} copy(bf16[4,8,96,768]{3,2,0,1:T(8,128)(2,1)} %all-to-all-done.2) | data formatting | bytes 9437184 | tf_op jit(solution)/shard_map/all_to_all | solution.py:82
  242.1 0.0 copy-done.1
  242.1 3.0 %fusion.18 = f32[256,768]{1,0:T(8,128)} fusion(bf16[3072,768]{1,0:T(8,128)(2,1)S(1)} %bitcast.28, s32[3072]{0:T(1024)S(1)} %select_n.41, f32[256]{0:T(256)S(1)} %maximum_convert_fusion), kind=kOutput, calls=%fused_computation.38 | convolution fusion | flops 1208942592 | bytes 5518336 | tf_op jit(solution)/shard_map/dot_general | solution.py:41
  (8 shorter events, 0.0 us)
Async XLA Ops:
  0.6 38.7 %copy-start = (bf16[1024,768]{1,0:T(8,128)(2,1)S(1)}, bf16[1024,768]{1,0:T(8,128)(2,1)}, u32[]{:S(2)}) copy-start(bf16[1024,768]{1,0:T(8,128)(2,1)} %param.10) | copy-start | bytes 4718596
  57.0 62.6 %collective-permute-start = (bf16[1,8,96,768]{3,2,1,0:T(8,128)(2,1)}, bf16[1,8,96,768]{3,2,1,0:T(8,128)(2,1)}, u32[]{:S(2)}, u32[]{:S(2)}) collective-permute-start(bf16[1,8,96,768]{3,2,1,0:T(8,128)(2,1)} %get-tuple-element.56), channel_id=1, source_target_pairs={{0,24},{8,0},{16,8},{24,16},{1,25},{9,1},{17,9},{25,17},{2,26},{10... | collective-permute-start | bytes 3538952 | tf_op jit(solution)/shard_map/ppermute | solution.py:14
  61.0 58.6 %collective-permute-start.1 = (bf16[1,8,96,768]{3,2,1,0:T(8,128)(2,1)}, bf16[1,8,96,768]{3,2,1,0:T(8,128)(2,1)}, u32[]{:S(2)}, u32[]{:S(2)}) collective-permute-start(bf16[1,8,96,768]{3,2,1,0:T(8,128)(2,1)} %get-tuple-element.55), channel_id=1, source_target_pairs={{0,16},{8,24},{16,0},{24,8},{1,17},{9,25},{17,1},{25,9},{2,18},{10... | collective-permute-start | bytes 3538952 | tf_op jit(solution)/shard_map/ppermute | solution.py:14
  61.5 58.2 %collective-permute-start.2 = (bf16[1,8,96,768]{3,2,1,0:T(8,128)(2,1)}, bf16[1,8,96,768]{3,2,1,0:T(8,128)(2,1)}, u32[]{:S(2)}, u32[]{:S(2)}) collective-permute-start(bf16[1,8,96,768]{3,2,1,0:T(8,128)(2,1)} %get-tuple-element.54), channel_id=1, source_target_pairs={{0,8},{8,16},{16,24},{24,0},{1,9},{9,17},{17,25},{25,1},{2,10},{10... | collective-permute-start | bytes 3538952 | tf_op jit(solution)/shard_map/ppermute | solution.py:14
  67.3 46.9 %all-to-all-start = ((s32[4,8,96]{2,1,0:T(8,128)}), s32[4,8,96]{2,1,0:T(8,128)S(1)}, u32[]{:S(2)}, u32[]{:S(2)}) async-start(s32[4,8,96]{2,1,0:T(8,128)} %reshape.51), calls=%async_computation | async-start | bytes 32768 | tf_op jit(solution)/shard_map/all_to_all | solution.py:90
  114.8 14.1 %all-to-all-start.1 = ((s32[4,8,96]{2,0,1:T(4,128)}), s32[4,8,96]{2,0,1:T(4,128)S(1)}, u32[]{:S(2)}, u32[]{:S(2)}) async-start(s32[4,8,96]{2,0,1:T(4,128)} %copy.24), calls=%async_computation.1 | async-start | bytes 32768 | tf_op jit(solution)/shard_map/all_to_all | solution.py:89
  128.8 6.7 %copy-start.2 = (s32[256]{0:T(256)S(1)}, s32[256]{0:T(256)}, u32[]{:S(2)}) copy-start(s32[256]{0:T(256)} %param.15) | copy-start | bytes 3076
  128.8 110.5 %all-to-all-start.2 = ((bf16[4,8,96,768]{3,2,0,1:T(8,128)(2,1)}), bf16[4,8,96,768]{3,2,0,1:T(8,128)(2,1)}, u32[]{:S(2)}, u32[]{:S(2)}) async-start(bf16[4,8,96,768]{3,2,0,1:T(8,128)(2,1)} %copy.29), calls=%async_computation.2 | async-start | bytes 9437184 | tf_op jit(solution)/shard_map/all_to_all | solution.py:82
  136.1 106.0 %copy-start.1 = (s32[256]{0:T(256)}, s32[256]{0:T(256)S(1)}, u32[]{:S(2)}) copy-start(s32[256]{0:T(256)S(1)} %get-tuple-element.52) | copy-start | bytes 3076
